TPU v7x, 512 devices: a whole 4x4x16 slice. The times are simulated.
512 devices in a mesh: grp: 8 (over y_lo, x), shard: 64 (over z, y_hi, core).
Axes of the slice: x: 4, y: 4 (y_hi: 2, y_lo: 2; y = y_hi * 2 + y_lo), z: 16, core: 2. Of those that a mesh axis runs over, the one named last changes fastest.
Arguments:
- window: bfloat16 [128, 4096], P('grp'), may hold values from -6 to 6
- weight: bfloat16 [11008, 4096], P('shard'), may hold values from -0.09375 to 0.09375
- factor_a: bfloat16 [1024, 4, 4096], P(('grp', 'shard')), may hold values from -6 to 6
- factor_b: bfloat16 [1024, 4, 11008], P(('grp', 'shard')), may hold values from -6 to 6
- fitness: float32 [1024], P(('grp', 'shard')), may hold values from -4 to 4
Outputs:
- perturbed: bfloat16 [11008, 16384], P('shard', 'grp')
- update: float32 [11008, 4096], P('shard', 'grp')
All inputs are finite; a program needn't handle non-finite values.
Results may differ from a plain program's by a relative error of at most 0.0029.
Values may be sent and summed in bfloat16 or wider, within the bound.
A program may use at most 64 MiB of HBM per device.

v0:
```python
import math
import jax
import jax.numpy as jnp
from jax import lax
from jax.sharding import Mesh
from jax.sharding import PartitionSpec as P

SHARD = ("shard_0", "shard_1", "shard_2")
GRP_SHARD = ("grp", "shard_0", "shard_1", "shard_2")


def side_by_side(arrays, axis, dim, along):
    columns = [a.reshape(*a.shape[:along], -1) for a in arrays]
    both = jnp.concatenate(columns, axis=along)
    filled, at, done = (lax.all_gather(both, axis, axis=dim, tiled=True), 0, [])
    for a, column in zip(arrays, columns):
        share = filled[..., at : at + column.shape[along]]
        done.append(share.reshape(*share.shape[:along], *a.shape[along:]))
        at += column.shape[along]
    return tuple(done)


def from_everyone(value, axis):
    peers = lax.axis_size(axis)
    return lax.all_to_all(
        jnp.broadcast_to(value[None], (peers, *value.shape)), axis, 0, 0, tiled=True
    )


def in_order(blocks, dim):
    blocks = jnp.moveaxis(blocks, 0, dim)
    dims = blocks.shape
    return blocks.reshape(*dims[:dim], dims[dim] * dims[dim + 1], *dims[dim + 2 :])


def gathered_copies(value, axis, dim):
    blocks = from_everyone(value, axis)
    return in_order(blocks, dim)


def stacked_from(value, axes, sequence):
    blocks = value[None]
    for k in sequence:
        blocks = lax.all_gather(blocks, axes[k], axis=0, tiled=True)
    block = [lax.axis_size(axes[k]) for k in reversed(sequence)]
    blocks = blocks.reshape(*block, *value.shape)
    turned = sorted(range(len(sequence)), key=lambda place: sequence[len(sequence) - 1 - place])
    return blocks.transpose(*turned, *range(len(sequence), blocks.ndim)).reshape(-1, *value.shape)


def gather_axes(value, axes, sequence, dim):
    return in_order(stacked_from(value, axes, sequence), dim)


def contract(left_rows, right_rows):
    return lax.dot_general(
        left_rows, right_rows, (((0,), (0,)), ((), ())), preferred_element_type=jnp.float32
    )


def local(window, weight, factor_a, factor_b, fitness):
    model_width = window.shape[1]
    cand_dev, factor_rank, _ = factor_a.shape
    shard_count = lax.axis_size(SHARD)
    total_cands = cand_dev * lax.axis_size("grp") * shard_count
    perturb = 0.25 / math.sqrt(model_width)
    step_scale = 0.5 / math.sqrt(total_cands)
    base_out = lax.dot_general(
        weight, window, (((1,), (1,)), ((), ())), preferred_element_type=jnp.float32
    )
    projected = jnp.einsum("td,crd->crt", window, factor_a, preferred_element_type=jnp.float32)
    projected_all, fitness_all = side_by_side((projected, fitness), SHARD, 0, 1)
    columns = lax.all_to_all(factor_b, SHARD, split_axis=2, concat_axis=0, tiled=True)
    col_width = columns.shape[2]
    low_rank = jnp.einsum(
        "crt,crf->fct", projected_all, columns.astype(jnp.float32), precision=lax.Precision.HIGHEST
    )
    perturbed = (
        (base_out[:, None, :] + perturb * low_rank).astype(jnp.bfloat16).reshape(col_width, -1)
    )
    weighted = (fitness_all[:, None, None] * columns.astype(jnp.float32)).astype(jnp.bfloat16)
    exchanged = lax.all_to_all(factor_a, "grp", split_axis=2, concat_axis=0, tiled=True)
    weighted_four = weighted.reshape(shard_count, cand_dev, factor_rank, col_width)
    weighted_flat = gathered_copies(weighted_four, "grp", 1).reshape(-1, col_width)
    owned_width = exchanged.shape[2]
    block_width = owned_width // 4
    update_parts = []
    for part_index in range(4):
        factor_slab = exchanged[:, :, part_index * block_width : (part_index + 1) * block_width]
        gathered = gather_axes(factor_slab, SHARD, (1, 0, 2), 0)
        update_parts.append(contract(weighted_flat, gathered.reshape(-1, block_width)))
    update = jnp.concatenate(update_parts, 1) * step_scale
    return (perturbed, update)


def solution(mesh):
    split = Mesh(
        mesh.devices.reshape(mesh.shape["grp"], 16, 2, 2), ("grp", "shard_0", "shard_1", "shard_2")
    )
    return jax.shard_map(
        local,
        mesh=split,
        in_specs=(
            P("grp", None),
            P(SHARD, None),
            P(GRP_SHARD, None, None),
            P(GRP_SHARD, None, None),
            P(GRP_SHARD),
        ),
        out_specs=(P(SHARD, "grp"), P(SHARD, "grp")),
        check_vma=False,
    )
```

profile of v0, /device:TPU:2, one launch (start us, length us, event | category | flops | bytes accessed | tf_op | source)
XLA Modules:
  0.0 370.6 jit_solution(10360211323301085646)
XLA Ops:
  7.2 4.5 %copy.56 = bf16[2,4,4096]{1,0,2:T(2,128)(2,1)S(1)} copy(bf16[2,4,4096]{2,1,0:T(4,128)(2,1)} %param.7) | data formatting | bytes 131072 | tf_op args[2]
  11.7 4.6 %reshape.55 = bf16[8,2,2048]{2,1,0:T(2,128)(2,1)} reshape(bf16[4096,2,4]{2,1,0:T(2,128)(2,1)S(1)} %bitcast.65) | data formatting | bytes 131072
  16.3 14.9 %all_to_all.41 = bf16[8,2,2048]{2,1,0:T(2,128)(2,1)} all-to-all(bf16[8,2,2048]{2,1,0:T(2,128)(2,1)} %reshape.55), channel_id=1, replica_groups=mesh['grp'=8,'shard_0'=16,'shard_1'=2,'shard_2'=2] {'grp'}, dimensions={0} | all-to-all | bytes 131072 | tf_op jit(solution)/shard_map/all_to_all | solution.py:82
  31.2 5.3 %reshape.56 = bf16[4096,2,4]{2,1,0:T(2,128)(2,1)S(1)} reshape(bf16[8,2,2048]{2,1,0:T(2,128)(2,1)} %all_to_all.41) | data formatting | bytes 131072
  36.5 3.3 copy.57
  40.6 5.9 %all-gather = bf16[32,4,128]{2,1,0:T(4,128)(2,1)S(1)} all-gather(bf16[16,4,128]{2,1,0:T(4,128)(2,1)S(1)} %get-tuple-element.12), channel_id=2, replica_groups=mesh['grp'=8,'shard_0'=16,'shard_1'=2,'shard_2'=2] {'shard_1'}, dimensions={0}, use_global_device_ids=true | all-gather | bytes 49152 | tf_op jit(solution)/shard_map/all_gather | solution.py:44
  46.5 36.9 %all_gather.41 = bf16[32,16,4,128]{3,1,2,0:T(8,128)(2,1)} all-gather(bf16[2,16,4,128]{3,1,2,0:T(8,128)(2,1)S(1)} %copy.58), channel_id=1, replica_groups=mesh['grp'=8,'shard_0'=16,'shard_1'=2,'shard_2'=2] {'shard_0'}, dimensions={0}, use_global_device_ids=true | all-gather | bytes 557056 | tf_op jit(solution)/shard_map/all_gather | solution.py:44
  83.5 5.9 %all-gather.1 = bf16[32,4,128]{2,1,0:T(4,128)(2,1)S(1)} all-gather(bf16[16,4,128]{2,1,0:T(4,128)(2,1)S(1)} %get-tuple-element.15), channel_id=3, replica_groups=mesh['grp'=8,'shard_0'=16,'shard_1'=2,'shard_2'=2] {'shard_1'}, dimensions={0}, use_global_device_ids=true | all-gather | bytes 49152 | tf_op jit(solution)/shard_map/all_gather | solution.py:44
  89.4 31.2 %all_gather.44 = bf16[32,16,4,128]{3,1,2,0:T(8,128)(2,1)} all-gather(bf16[2,16,4,128]{3,1,2,0:T(8,128)(2,1)S(1)} %copy.60), channel_id=1, replica_groups=mesh['grp'=8,'shard_0'=16,'shard_1'=2,'shard_2'=2] {'shard_0'}, dimensions={0}, use_global_device_ids=true | all-gather | bytes 557056 | tf_op jit(solution)/shard_map/all_gather | solution.py:44
  120.7 9.1 %copy.52 = bf16[2,4,11008]{1,0,2:T(2,128)(2,1)} copy(bf16[2,4,11008]{2,1,0:T(4,128)(2,1)S(1)} %copy-done.6) | data formatting | bytes 352256 | tf_op args[3]
  129.8 11.3 %reshape.53 = bf16[64,2,688]{2,1,0:T(2,128)(2,1)} reshape(bf16[11008,2,4]{2,1,0:T(2,128)(2,1)} %bitcast.62) | data formatting | bytes 352256
  141.0 11.0 %all-to-all-start = ((bf16[64,2,688]{2,1,0:T(2,128)(2,1)}), bf16[64,2,688]{2,1,0:T(2,128)(2,1)S(1)}, u32[]{:S(2)}, u32[]{:S(2)}) async-start(bf16[64,2,688]{2,1,0:T(2,128)(2,1)} %reshape.53), calls=%async_computation | async-start | bytes 393216 | tf_op jit(solution)/shard_map/all_to_all | solution.py:73
  152.1 5.9 %all-gather.2 = bf16[32,4,128]{2,1,0:T(4,128)(2,1)S(1)} all-gather(bf16[16,4,128]{2,1,0:T(4,128)(2,1)S(1)} %get-tuple-element.14), channel_id=4, replica_groups=mesh['grp'=8,'shard_0'=16,'shard_1'=2,'shard_2'=2] {'shard_1'}, dimensions={0}, use_global_device_ids=true | all-gather | bytes 49152 | tf_op jit(solution)/shard_map/all_gather | solution.py:44
  158.0 34.8 %all_gather.47 = bf16[32,16,4,128]{3,1,2,0:T(8,128)(2,1)} all-gather(bf16[2,16,4,128]{3,1,2,0:T(8,128)(2,1)S(1)} %copy.62), channel_id=1, replica_groups=mesh['grp'=8,'shard_0'=16,'shard_1'=2,'shard_2'=2] {'shard_0'}, dimensions={0}, use_global_device_ids=true | all-gather | bytes 557056 | tf_op jit(solution)/shard_map/all_gather | solution.py:44
  193.4 75.5 %all-gather.4 = f32[64,2,65]{2,1,0:T(2,128)S(1)} all-gather(f32[1,2,65]{2,1,0:T(2,128)S(1)} %maximum_bitcast_fusion), channel_id=1, replica_groups=mesh['grp'=8,'shard_0'=16,'shard_1'=2,'shard_2'=2] {'shard_0','shard_1',..., dimensions={0}, use_global_device_ids=true | all-gather | bytes 33800 | tf_op jit(solution)/shard_map/all_gather | solution.py:15
  269.8 5.9 %all-gather.3 = bf16[32,4,128]{2,1,0:T(4,128)(2,1)S(1)} all-gather(bf16[16,4,128]{2,1,0:T(4,128)(2,1)S(1)} %get-tuple-element.13), channel_id=5, replica_groups=mesh['grp'=8,'shard_0'=16,'shard_1'=2,'shard_2'=2] {'shard_1'}, dimensions={0}, use_global_device_ids=true | all-gather | bytes 49152 | tf_op jit(solution)/shard_map/all_gather | solution.py:44
  276.3 6.3 %reshape.54 = bf16[11008,2,4]{2,1,0:T(2,128)(2,1)} reshape(bf16[64,2,688]{2,1,0:T(2,128)(2,1)S(1)} %all-to-all-done) | data formatting | bytes 352256
  282.6 10.4 %copy.53 = bf16[2,4,64,172]{3,1,0,2:T(4,128)(2,1)S(1)} copy(bf16[2,4,64,172]{1,0,3,2:T(2,128)(2,1)} %bitcast.61) | data formatting | bytes 352256 | tf_op jit(solution)/shard_map/all_to_all | solution.py:73
  293.2 1.9 broadcast_in_dim.18
  295.1 4.8 %all-to-all-start.1 = ((bf16[8,64,2,4,172]{4,3,2,1,0:T(4,128)(2,1)}), bf16[8,64,2,4,172]{4,3,2,1,0:T(4,128)(2,1)S(1)}, u32[]{:S(2)}, u32[]{:S(2)}) async-start(bf16[8,64,2,4,172]{4,3,2,1,0:T(4,128)(2,1)} %broadcast_in_dim.18), calls=%async_computation.1 | async-start | bytes 4194304 | tf_op jit(solution)/shard_map/all_to_all | solution.py:25
  299.9 31.9 %all_gather.50 = bf16[32,16,4,128]{3,1,2,0:T(8,128)(2,1)} all-gather(bf16[2,16,4,128]{3,1,2,0:T(8,128)(2,1)} %copy.64), channel_id=1, replica_groups=mesh['grp'=8,'shard_0'=16,'shard_1'=2,'shard_2'=2] {'shard_0'}, dimensions={0}, use_global_device_ids=true | all-gather | bytes 557056 | tf_op jit(solution)/shard_map/all_gather | solution.py:44
  331.8 1.5 copy.51
  333.3 1.6 copy.54
  336.3 3.1 fusion
  339.4 2.2 copy.66
  341.6 2.8 copy.59
  344.4 2.8 copy.61
  347.2 2.8 copy.63
  350.0 2.8 copy.65
  352.8 2.5 copy.55
  355.3 3.1 reshape_reshape.3
  358.4 2.1 fusion.5
  (51 shorter events, 8.2 us)
Async XLA Ops:
  7.2 327.8 %copy-start = (bf16[172,4096]{1,0:T(8,128)(2,1)S(1)}, bf16[172,4096]{1,0:T(8,128)(2,1)}, u32[]{:S(2)}) copy-start(bf16[172,4096]{1,0:T(8,128)(2,1)} %param.6) | copy-start | bytes 4227076
  7.2 334.4 %all-gather.10.cloned.1.call-start = ((), (), s32[]{:S(2)}) async-start(), calls=%async_computation.3 | async-start | bytes 1572864 | tf_op jit(solution)/shard_map/all_gather | solution.py:44
  39.8 80.9 %copy-start.6 = (bf16[2,4,11008]{2,1,0:T(4,128)(2,1)S(1)}, bf16[2,4,11008]{2,1,0:T(4,128)(2,1)}, u32[]{:S(2)}) copy-start(bf16[2,4,11008]{2,1,0:T(4,128)(2,1)} %param.8) | copy-start | bytes 528388
  83.4 260.9 %all-gather.12.cloned.1.call-start = ((), (), s32[]{:S(2)}) async-start(), calls=%async_computation.4 | async-start | bytes 1572864 | tf_op jit(solution)/shard_map/all_gather | solution.py:44
  129.8 63.1 %copy-start.7 = (bf16[16,4096]{1,0:T(8,128)(2,1)S(1)}, bf16[16,4096]{1,0:T(8,128)(2,1)}, u32[]{:S(2)}) copy-start(bf16[16,4096]{1,0:T(8,128)(2,1)} %param.5) | copy-start | bytes 393220
  129.8 63.1 %copy-start.8 = (bf16[2,4,4096]{2,1,0:T(4,128)(2,1)S(1)}, bf16[2,4,4096]{2,1,0:T(4,128)(2,1)}, u32[]{:S(2)}) copy-start(bf16[2,4,4096]{2,1,0:T(4,128)(2,1)} %param.7) | copy-start | bytes 196612
  129.8 63.4 %copy-start.9 = (f32[2]{0:T(128)S(1)}, f32[2]{0:T(128)}, u32[]{:S(2)}) copy-start(f32[2]{0:T(128)} %param.9) | copy-start | bytes 28
  141.0 135.3 %all-to-all-start = ((bf16[64,2,688]{2,1,0:T(2,128)(2,1)}), bf16[64,2,688]{2,1,0:T(2,128)(2,1)S(1)}, u32[]{:S(2)}, u32[]{:S(2)}) async-start(bf16[64,2,688]{2,1,0:T(2,128)(2,1)} %reshape.53), calls=%async_computation | async-start | bytes 393216 | tf_op jit(solution)/shard_map/all_to_all | solution.py:73
  152.0 195.2 %all-gather.14.cloned.1.call-start = ((), (), s32[]{:S(2)}) async-start(), calls=%async_computation.5 | async-start | bytes 1572864 | tf_op jit(solution)/shard_map/all_gather | solution.py:44
  268.9 0.6 copy-start.5
  293.0 2.1 copy-start.4
  295.1 57.7 %all-to-all-start.1 = ((bf16[8,64,2,4,172]{4,3,2,1,0:T(4,128)(2,1)}), bf16[8,64,2,4,172]{4,3,2,1,0:T(4,128)(2,1)S(1)}, u32[]{:S(2)}, u32[]{:S(2)}) async-start(bf16[8,64,2,4,172]{4,3,2,1,0:T(4,128)(2,1)} %broadcast_in_dim.18), calls=%async_computation.1 | async-start | bytes 4194304 | tf_op jit(solution)/shard_map/all_to_all | solution.py:25
  299.9 50.1 %all-gather.16.cloned.1.call-start = ((), (), s32[]{:S(2)}) async-start(), calls=%async_computation.6 | async-start | bytes 1572864 | tf_op jit(solution)/shard_map/all_gather | solution.py:44
  358.4 2.1 copy-start.1
  360.5 1.2 copy-start.2
  361.3 1.3 copy-start.3
Sparse Core Ops, SparseCore 0:
  83.6 14.1 all-gather.9
  120.8 15.1 all-gather.11
  193.0 17.0 all-gather.13
  331.9 15.6 all-gather.15
where the time goes:
time: 372 us; the launch traced here: 371 us
  blocking collectives  249 us (67%)
  local copies, waits for them, and re-layouts  81.7 us (22%)
  starting transfers between devices  15.9 us (4%)
  between operations  13.9 us (4%)
  matrix products  9.06 us (2%)
    all_gather x8, blocking collectives, stacked_from(): blocks = lax.all_gather(blocks, axes[k], axis=0, tiled=True)  159 us
    all_gather x1, blocking collectives, side_by_side(): filled, at, done = (lax.all_gather(both, axis, axis=dim, tiled=True), 0, [])  75.5 us
    unnamed x27, local copies, waits for them, and re-layouts  44.3 us
    all_to_all x1, blocking collectives, local(): lax.all_to_all(factor_a, 'grp', split_axis=2, concat_axis=0, tiled=True)  14.9 us
    transpose x4, local copies, waits for them, and re-layouts, stacked_from(): blocks.transpose(*turned, *range(len(sequence), blocks.ndim))  11.1 us
    all_to_all x1, starting transfers between devices, local(): lax.all_to_all(factor_b, SHARD, split_axis=2, concat_axis=0, tiled=True)  11 us
    all_to_all x1, local copies, waits for them, and re-layouts, local(): lax.all_to_all(factor_b, SHARD, split_axis=2, concat_axis=0, tiled=True)  10.4 us
  transfers between devices with their start and end apart: 6, of which 0 were waited for; matrix products, arithmetic and copies ran while one was open for 17% of the time, Pallas kernels for 0%

commit v1 on v0

--- a/solution.py
+++ b/solution.py
@@ -41,7 +41,13 @@
 def stacked_from(value, axes, sequence):
     blocks = value[None]
     for k in sequence:
-        blocks = lax.all_gather(blocks, axes[k], axis=0, tiled=True)
+        own_rows = axes[k]
+        blocks = jnp.concatenate(
+            lax.all_to_all(
+                jnp.stack([blocks for _ in range(lax.axis_size(own_rows))], axis=0), own_rows, 0, 0
+            ),
+            axis=0,
+        )
     block = [lax.axis_size(axes[k]) for k in reversed(sequence)]
     blocks = blocks.reshape(*block, *value.shape)
     turned = sorted(range(len(sequence)), key=lambda place: sequence[len(sequence) - 1 - place])

time: 372 us -> 419 us (1.13)
  the two profiles are of different devices: /device:TPU:2 before, /device:TPU:39 now
where the time goes in v1:
time: 419 us; the launch traced here: 416 us
  blocking collectives  234 us (56%)
  local copies, waits for them, and re-layouts  77.1 us (18%)
  starting transfers between devices  44.4 us (11%)
  waiting for transfers between devices  36.7 us (9%)
  other arithmetic  13 us (3%)
  matrix products  9.74 us (2%)
    all_to_all x6, blocking collectives, stacked_from(): lax.all_to_all(jnp.stack([blocks for _ in range(lax.axis_size(own_rows))]...  92.1 us
    all_gather x1, blocking collectives, side_by_side(): filled, at, done = (lax.all_gather(both, axis, axis=dim, tiled=True), 0, [])  88.8 us
    unnamed x41, local copies, waits for them, and re-layouts  45.2 us
    all_to_all x1, blocking collectives, local(): lax.all_to_all(factor_b, SHARD, split_axis=2, concat_axis=0, tiled=True)  44.3 us
    all_to_all x6, starting transfers between devices, stacked_from(): lax.all_to_all(jnp.stack([blocks for _ in range(lax.axis_size(own_rows))]...  39.2 us
    all_to_all x1, waiting for transfers between devices, from_everyone(): lax.all_to_all(jnp.broadcast_to(value[None], (peers, *value.shape)), axis...  22.9 us
    all_to_all x6, waiting for transfers between devices, stacked_from(): lax.all_to_all(jnp.stack([blocks for _ in range(lax.axis_size(own_rows))]...  13.8 us
    another operation x8, other arithmetic, stacked_from(): jnp.stack([blocks for _ in range(lax.axis_size(own_rows))], axis=0)  12 us
  transfers between devices with their start and end apart: 7, of which 5 were waited for; matrix products, arithmetic and copies ran while one was open for 17% of the time, Pallas kernels for 0%

profile of v1, /device:TPU:39, one launch (start us, length us, event | category | flops | bytes accessed | tf_op | source)
XLA Modules:
  0.0 415.9 jit_solution(3959636218383301764)
XLA Ops:
  0.6 4.5 %copy.37 = bf16[2,4,4096]{1,0,2:T(2,128)(2,1)S(1)} copy(bf16[2,4,4096]{2,1,0:T(4,128)(2,1)} %param.7) | data formatting | bytes 131072 | tf_op args[2]
  5.1 4.6 %reshape.43 = bf16[8,2,2048]{2,1,0:T(2,128)(2,1)} reshape(bf16[4096,2,4]{2,1,0:T(2,128)(2,1)S(1)} %bitcast.77) | data formatting | bytes 131072
  9.7 8.8 %all_to_all.101 = bf16[8,2,2048]{2,1,0:T(2,128)(2,1)} all-to-all(bf16[8,2,2048]{2,1,0:T(2,128)(2,1)} %reshape.43), channel_id=1, replica_groups=mesh['grp'=8,'shard_0'=16,'shard_1'=2,'shard_2'=2] {'grp'}, dimensions={0} | all-to-all | bytes 131072 | tf_op jit(solution)/shard_map/all_to_all | solution.py:88
  18.6 5.3 %reshape.44 = bf16[4096,2,4]{2,1,0:T(2,128)(2,1)S(1)} reshape(bf16[8,2,2048]{2,1,0:T(2,128)(2,1)} %all_to_all.101) | data formatting | bytes 131072
  23.8 3.3 copy.38
  28.6 3.9 all-to-all-start.3
  33.1 3.7 all-to-all-done.3
  36.7 3.3 all-to-all-start.6
  40.6 3.7 all-to-all-done.6
  44.3 3.3 all-to-all-start.9
  48.2 3.7 all-to-all-done.9
  51.8 3.3 all-to-all-start.12
  55.1 11.0 %copy.33 = bf16[2,4,11008]{1,0,2:T(2,128)(2,1)} copy(bf16[2,4,11008]{2,1,0:T(4,128)(2,1)} %param.8) | data formatting | bytes 352256 | tf_op args[3]
  66.1 10.6 %reshape.41 = bf16[64,2,688]{2,1,0:T(2,128)(2,1)S(1)} reshape(bf16[11008,2,4]{2,1,0:T(2,128)(2,1)} %bitcast.74) | data formatting | bytes 352256
  76.7 44.3 %all_to_all.102 = bf16[64,2,688]{2,1,0:T(2,128)(2,1)S(1)} all-to-all(bf16[64,2,688]{2,1,0:T(2,128)(2,1)S(1)} %reshape.41), channel_id=1, replica_groups=mesh['grp'=8,'shard_0'=16,'shard_1'=2,'shard_2'=2] {'shard_0','shard_1',..., dimensions={0} | all-to-all | bytes 352256 | tf_op jit(solution)/shard_map/all_to_all | solution.py:79
  121.3 31.2 %all_to_all.103 = bf16[16,2,16,4,128]{4,3,2,1,0:T(4,128)(2,1)} all-to-all(bf16[16,2,16,4,128]{4,3,2,1,0:T(4,128)(2,1)S(1)} %stack.37), channel_id=1, replica_groups=mesh['grp'=8,'shard_0'=16,'shard_1'=2,'shard_2'=2] {'shard_0'}, dimensions={0} | all-to-all | bytes 1048576 | tf_op jit(solution)/shard_map/all_to_all | solution.py:46
  152.7 33.7 %all_to_all.104 = bf16[16,2,16,4,128]{4,3,2,1,0:T(4,128)(2,1)} all-to-all(bf16[16,2,16,4,128]{4,3,2,1,0:T(4,128)(2,1)S(1)} %stack.40), channel_id=1, replica_groups=mesh['grp'=8,'shard_0'=16,'shard_1'=2,'shard_2'=2] {'shard_0'}, dimensions={0} | all-to-all | bytes 1048576 | tf_op jit(solution)/shard_map/all_to_all | solution.py:46
  187.5 10.2 %all-to-all-start.10 = ((bf16[16,2,16,4,128]{4,3,2,1,0:T(4,128)(2,1)}), bf16[16,2,16,4,128]{4,3,2,1,0:T(4,128)(2,1)S(1)}, u32[]{:S(2)}, u32[]{:S(2)}) async-start(bf16[16,2,16,4,128]{4,3,2,1,0:T(4,128)(2,1)} %stack.43), calls=%async_computation.10 | async-start | bytes 1048576 | tf_op jit(solution)/shard_map/all_to_all | solution.py:46
  198.2 88.8 %all-gather = f32[64,2,65]{2,1,0:T(2,128)S(1)} all-gather(f32[1,2,65]{2,1,0:T(2,128)S(1)} %maximum_bitcast_fusion), channel_id=1, replica_groups=mesh['grp'=8,'shard_0'=16,'shard_1'=2,'shard_2'=2] {'shard_0','shard_1',..., dimensions={0}, use_global_device_ids=true | all-gather | bytes 33800 | tf_op jit(solution)/shard_map/all_gather | solution.py:15
  287.9 6.3 %reshape.42 = bf16[11008,2,4]{2,1,0:T(2,128)(2,1)} reshape(bf16[64,2,688]{2,1,0:T(2,128)(2,1)S(1)} %all_to_all.102) | data formatting | bytes 352256
  294.2 10.4 %copy.34 = bf16[2,4,64,172]{3,1,0,2:T(4,128)(2,1)S(1)} copy(bf16[2,4,64,172]{1,0,3,2:T(2,128)(2,1)} %bitcast.73) | data formatting | bytes 352256 | tf_op jit(solution)/shard_map/all_to_all | solution.py:79
  306.7 5.2 %all-to-all-start.1 = ((bf16[8,64,2,4,172]{4,3,2,1,0:T(4,128)(2,1)}), bf16[8,64,2,4,172]{4,3,2,1,0:T(4,128)(2,1)S(1)}, u32[]{:S(2)}, u32[]{:S(2)}) async-start(bf16[8,64,2,4,172]{4,3,2,1,0:T(4,128)(2,1)} %broadcast_in_dim.2), calls=%async_computation.1 | async-start | bytes 4194304 | tf_op jit(solution)/shard_map/all_to_all | solution.py:25
  311.9 3.0 pad_maximum_fusion
  314.9 3.0 pad_maximum_fusion.1
  319.4 22.9 %all-to-all-done.1 = bf16[8,64,2,4,172]{4,3,2,1,0:T(4,128)(2,1)S(1)} async-done(((bf16[8,64,2,4,172]{4,3,2,1,0:T(4,128)(2,1)}), bf16[8,64,2,4,172]{4,3,2,1,0:T(4,128)(2,1)S(1)}, u32[]{:S(2)}, u32[]{:S(2)}) %all-to-all-start.1) | async-done | bytes 1409056 | tf_op jit(solution)/shard_map/all_to_all | solution.py:25
  342.2 7.4 %all_to_all.105 = bf16[2,32,16,4,128]{4,3,2,1,0:T(4,128)(2,1)} all-to-all(bf16[2,32,16,4,128]{4,3,2,1,0:T(4,128)(2,1)} %pad_maximum_fusion), channel_id=1, replica_groups=mesh['grp'=8,'shard_0'=16,'shard_1'=2,'shard_2'=2] {'shard_2'}, dimensions={0} | all-to-all | bytes 2097152 | tf_op jit(solution)/shard_map/all_to_all | solution.py:46
  349.7 5.5 %all_to_all.106 = bf16[2,32,16,4,128]{4,3,2,1,0:T(4,128)(2,1)} all-to-all(bf16[2,32,16,4,128]{4,3,2,1,0:T(4,128)(2,1)S(1)} %copy-done.3), channel_id=1, replica_groups=mesh['grp'=8,'shard_0'=16,'shard_1'=2,'shard_2'=2] {'shard_2'}, dimensions={0} | all-to-all | bytes 2097152 | tf_op jit(solution)/shard_map/all_to_all | solution.py:46
  355.2 5.4 %all_to_all.107 = bf16[2,32,16,4,128]{4,3,2,1,0:T(4,128)(2,1)} all-to-all(bf16[2,32,16,4,128]{4,3,2,1,0:T(4,128)(2,1)S(1)} %copy-done.4), channel_id=1, replica_groups=mesh['grp'=8,'shard_0'=16,'shard_1'=2,'shard_2'=2] {'shard_2'}, dimensions={0} | all-to-all | bytes 2097152 | tf_op jit(solution)/shard_map/all_to_all | solution.py:46
  361.6 15.3 %all-to-all-start.13 = ((bf16[16,2,16,4,128]{4,3,2,1,0:T(4,128)(2,1)}), bf16[16,2,16,4,128]{4,3,2,1,0:T(4,128)(2,1)}, u32[]{:S(2)}, u32[]{:S(2)}) async-start(bf16[16,2,16,4,128]{4,3,2,1,0:T(4,128)(2,1)} %stack.46), calls=%async_computation.13 | async-start | bytes 1048576 | tf_op jit(solution)/shard_map/all_to_all | solution.py:46
  381.4 3.2 fusion
  389.2 3.1 reshape_reshape.15
  404.6 8.9 %all_to_all.108 = bf16[2,32,16,4,128]{4,3,2,1,0:T(4,128)(2,1)S(1)} all-to-all(bf16[2,32,16,4,128]{4,3,2,1,0:T(4,128)(2,1)S(1)} %pad_maximum_fusion.3), channel_id=1, replica_groups=mesh['grp'=8,'shard_0'=16,'shard_1'=2,'shard_2'=2] {'shard_2'}, dimensions={0} | all-to-all | bytes 2097152 | tf_op jit(solution)/shard_map/all_to_all | solution.py:46
  (70 shorter events, 34.6 us)
Async XLA Ops:
  0.6 379.4 %copy-start = (bf16[172,4096]{1,0:T(8,128)(2,1)S(1)}, bf16[172,4096]{1,0:T(8,128)(2,1)}, u32[]{:S(2)}) copy-start(bf16[172,4096]{1,0:T(8,128)(2,1)} %param.6) | copy-start | bytes 4227076
  28.6 8.2 %all-to-all-start.3 = ((bf16[2,1,16,4,128]{4,3,2,1,0:T(4,128)(2,1)}), bf16[2,1,16,4,128]{4,3,2,1,0:T(4,128)(2,1)S(1)}, u32[]{:S(2)}, u32[]{:S(2)}) async-start(bf16[2,1,16,4,128]{4,3,2,1,0:T(4,128)(2,1)} %pad_maximum_fusion.4), calls=%async_computation.3 | async-start | bytes 65536 | tf_op jit(solution)/shard_map/all_to_all | solution.py:46
  36.7 7.6 %all-to-all-start.6 = ((bf16[2,1,16,4,128]{4,3,2,1,0:T(4,128)(2,1)}), bf16[2,1,16,4,128]{4,3,2,1,0:T(4,128)(2,1)S(1)}, u32[]{:S(2)}, u32[]{:S(2)}) async-start(bf16[2,1,16,4,128]{4,3,2,1,0:T(4,128)(2,1)} %pad_maximum_fusion.5), calls=%async_computation.6 | async-start | bytes 65536 | tf_op jit(solution)/shard_map/all_to_all | solution.py:46
  44.3 7.6 %all-to-all-start.9 = ((bf16[2,1,16,4,128]{4,3,2,1,0:T(4,128)(2,1)}), bf16[2,1,16,4,128]{4,3,2,1,0:T(4,128)(2,1)S(1)}, u32[]{:S(2)}, u32[]{:S(2)}) async-start(bf16[2,1,16,4,128]{4,3,2,1,0:T(4,128)(2,1)} %pad_maximum_fusion.6), calls=%async_computation.9 | async-start | bytes 65536 | tf_op jit(solution)/shard_map/all_to_all | solution.py:46
  51.8 24.9 %all-to-all-start.12 = ((bf16[2,1,16,4,128]{4,3,2,1,0:T(4,128)(2,1)}), bf16[2,1,16,4,128]{4,3,2,1,0:T(4,128)(2,1)S(1)}, u32[]{:S(2)}, u32[]{:S(2)}) async-start(bf16[2,1,16,4,128]{4,3,2,1,0:T(4,128)(2,1)} %pad_maximum_fusion.7), calls=%async_computation.12 | async-start | bytes 65536 | tf_op jit(solution)/shard_map/all_to_all | solution.py:46
  76.7 110.8 %copy-start.13 = (bf16[2,1,16,4,128]{4,3,2,1,0:T(4,128)(2,1)}, bf16[2,1,16,4,128]{4,3,2,1,0:T(4,128)(2,1)S(1)}, u32[]{:S(2)}) copy-start(bf16[2,1,16,4,128]{4,3,2,1,0:T(4,128)(2,1)S(1)} %all-to-all-done.12) | copy-start | bytes 98308
  121.2 76.5 %copy-start.12 = (bf16[16,4096]{1,0:T(8,128)(2,1)S(1)}, bf16[16,4096]{1,0:T(8,128)(2,1)}, u32[]{:S(2)}) copy-start(bf16[16,4096]{1,0:T(8,128)(2,1)} %param.5) | copy-start | bytes 393220
  121.2 76.5 %copy-start.15 = (bf16[2,4,4096]{2,1,0:T(4,128)(2,1)S(1)}, bf16[2,4,4096]{2,1,0:T(4,128)(2,1)}, u32[]{:S(2)}) copy-start(bf16[2,4,4096]{2,1,0:T(4,128)(2,1)} %param.7) | copy-start | bytes 196612
  121.3 76.8 %copy-start.16 = (f32[2]{0:T(128)S(1)}, f32[2]{0:T(128)}, u32[]{:S(2)}) copy-start(f32[2]{0:T(128)} %param.9) | copy-start | bytes 28
  187.5 117.3 %all-to-all-start.10 = ((bf16[16,2,16,4,128]{4,3,2,1,0:T(4,128)(2,1)}), bf16[16,2,16,4,128]{4,3,2,1,0:T(4,128)(2,1)S(1)}, u32[]{:S(2)}, u32[]{:S(2)}) async-start(bf16[16,2,16,4,128]{4,3,2,1,0:T(4,128)(2,1)} %stack.43), calls=%async_computation.10 | async-start | bytes 1048576 | tf_op jit(solution)/shard_map/all_to_all | solution.py:46
  287.0 0.6 copy-start.8
  304.6 2.1 copy-start.7
  304.8 1.9 copy-start.5
  306.7 35.5 %all-to-all-start.1 = ((bf16[8,64,2,4,172]{4,3,2,1,0:T(4,128)(2,1)}), bf16[8,64,2,4,172]{4,3,2,1,0:T(4,128)(2,1)S(1)}, u32[]{:S(2)}, u32[]{:S(2)}) async-start(bf16[8,64,2,4,172]{4,3,2,1,0:T(4,128)(2,1)} %broadcast_in_dim.2), calls=%async_computation.1 | async-start | bytes 4194304 | tf_op jit(solution)/shard_map/all_to_all | solution.py:25
  311.9 6.0 %copy-start.6 = (bf16[16,2,16,4,128]{4,3,2,1,0:T(4,128)(2,1)S(1)}, bf16[16,2,16,4,128]{4,3,2,1,0:T(4,128)(2,1)}, u32[]{:S(2)}) copy-start(bf16[16,2,16,4,128]{4,3,2,1,0:T(4,128)(2,1)} %copy-done.5) | copy-start | bytes 1572868
  342.2 7.4 %copy-start.3 = (bf16[2,32,16,4,128]{4,3,2,1,0:T(4,128)(2,1)S(1)}, bf16[2,32,16,4,128]{4,3,2,1,0:T(4,128)(2,1)}, u32[]{:S(2)}) copy-start(bf16[2,32,16,4,128]{4,3,2,1,0:T(4,128)(2,1)} %pad_maximum_fusion.1) | copy-start | bytes 3145732
  342.2 12.9 %copy-start.4 = (bf16[2,32,16,4,128]{4,3,2,1,0:T(4,128)(2,1)S(1)}, bf16[2,32,16,4,128]{4,3,2,1,0:T(4,128)(2,1)}, u32[]{:S(2)}) copy-start(bf16[2,32,16,4,128]{4,3,2,1,0:T(4,128)(2,1)} %pad_maximum_fusion.2) | copy-start | bytes 3145732
  349.7 10.9 %copy-start.14 = (bf16[2,1,16,4,128]{4,3,2,1,0:T(4,128)(2,1)S(1)}, bf16[2,1,16,4,128]{4,3,2,1,0:T(4,128)(2,1)}, u32[]{:S(2)}) copy-start(bf16[2,1,16,4,128]{4,3,2,1,0:T(4,128)(2,1)} %copy-done.13) | copy-start | bytes 98308
  361.6 41.1 %all-to-all-start.13 = ((bf16[16,2,16,4,128]{4,3,2,1,0:T(4,128)(2,1)}), bf16[16,2,16,4,128]{4,3,2,1,0:T(4,128)(2,1)}, u32[]{:S(2)}, u32[]{:S(2)}) async-start(bf16[16,2,16,4,128]{4,3,2,1,0:T(4,128)(2,1)} %stack.46), calls=%async_computation.13 | async-start | bytes 1048576 | tf_op jit(solution)/shard_map/all_to_all | solution.py:46
  392.4 1.9 copy-start.1
  392.4 2.5 copy-start.2
  414.2 0.9 copy-start.9
  414.2 0.9 copy-start.10
  414.2 1.0 copy-start.11
